TPU v7x, 32 devices: a whole 2x2x4 slice. The times are simulated.
32 devices in a mesh: row: 8 (over z, y), col: 4 (over x, core).
Axes of the slice: x: 2, y: 2, z: 4, core: 2. Of those that a mesh axis runs over, the one named last changes fastest.
Arguments:
- matrix_tiles: float32 [8, 4, 16, 256, 256], P('row', 'col'), may hold values from -0.3125 to 0.3125
- tile_slot: int32 [8, 4, 16], P('row', 'col'), may hold values from 0 to 2047, as said below
- cost_vector: float32 [512, 256], P('col'), may hold values from -24 to 24
- lower_bound: float32 [512, 256], P('col'), may hold values from -4 to 4
- bound_width: float32 [512, 256], P('col'), may hold values from 0.5 to 4
- variable_kind: int32 [512, 256], P('col'), may hold values from 0 to 2
- right_side: float32 [128, 256], P('row'), may hold values from -24 to 24
- row_kind: int32 [128, 256], P('row'), may hold values from 0 to 1
- primal_start: float32 [512, 256], P('col'), may hold values from -6 to 6
- dual_start: float32 [128, 256], P('row'), may hold values from -3 to 3
- primal_weight: float32 [], replicated, may hold values from 0.7 to 1.4
- step_start: float32 [], replicated, may hold values from 1 to 2
Outputs:
- primal: float32 [512, 256], P('col')
- dual: float32 [128, 256], P('row')
Inputs may be any that keep to these rules, and one draw needn't show every extreme that they name: `tile_slot`: within each block [r, c] the 16 tiles lie in different column tiles. Split a block's 128 column tiles into runs of 16 in a row: no run holds more than 2 of the block's tiles.
All inputs are finite; a program needn't handle non-finite values.
Results may differ from a plain program's by a relative error of at most 0.00026.
Values sent between devices are 32-bit elements; how exact they have to be, the bound alone decides.
No kernel may reach another device: no remote copies, remote signals or barrier semaphores. Data moves between devices by JAX's collectives and lax.ppermute only.
A program may use at most 64 MiB of HBM per device.

v0:
```python
import jax
import jax.numpy as jnp
from jax import lax
from jax.sharding import PartitionSpec as P

ITERS = 4
highest = lax.Precision.HIGHEST


def project_primal(values, lower_bound, bound_width, variable_kind):
    lifted = jnp.where(variable_kind >= 1, jnp.maximum(values, lower_bound), values)
    return jnp.where(variable_kind == 2, jnp.minimum(lifted, lower_bound + bound_width), lifted)


def project_dual(values, row_kind):
    return jnp.where(row_kind == 1, jnp.maximum(values, 0.0), values)


def next_step(cross, dual_square, primal_square, weight, step_size, iteration):
    movement = 0.5 * weight * primal_square + 0.5 * dual_square / weight
    count = iteration + 11.0
    return movement / jnp.maximum(
        jnp.abs(cross) / (1.0 - count ** (-0.3)), movement / ((1.0 + count ** (-0.6)) * step_size)
    )


def shards(
    matrix_tiles,
    tile_slot,
    cost_vector,
    lower_bound,
    bound_width,
    variable_kind,
    right_side,
    row_kind,
    primal_start,
    dual_start,
    primal_weight,
    step_start,
):
    tile_set = matrix_tiles[0, 0]
    slots = tile_slot[0, 0]
    row_tiles, tile_width = right_side.shape
    col_tiles = cost_vector.shape[0]
    tile_count = slots.shape[0]
    row_count = lax.axis_size("row")
    row_of = slots // col_tiles
    col_of = slots % col_tiles
    row_onehot = (row_of[None, :] == jnp.arange(row_tiles, dtype=jnp.int32)[:, None]).astype(
        jnp.float32
    )

    def forward_picked(picked):
        product = jnp.einsum("tij,tj->ti", tile_set, picked, precision=highest)
        partial_rows = jnp.dot(row_onehot, product, precision=highest)
        return lax.psum(partial_rows, "col")

    def backward_product(vector):
        picked = vector[row_of]
        return jnp.einsum("tij,ti->tj", tile_set, picked, precision=highest)

    share_len = col_tiles * tile_width // row_count
    offset = lax.axis_index("row") * share_len

    def take_share(values):
        return lax.dynamic_slice_in_dim(values.reshape(-1), offset, share_len, 0)

    share_tiles = col_tiles // row_count
    capacity = (tile_count + row_count - 1) // row_count
    share_of = col_of // share_tiles
    counter = jnp.arange(tile_count, dtype=jnp.int32)
    earlier = (counter[None, :] < counter[:, None]) & (share_of[None, :] == share_of[:, None])
    position = jnp.sum(earlier.astype(jnp.int32), axis=1)
    destination = share_of * capacity + position
    send_hit = destination[None, :] == jnp.arange(row_count * capacity, dtype=jnp.int32)[:, None]
    send_onehot = send_hit.astype(jnp.float32)
    local_index = col_of % share_tiles
    occupied = jnp.sum(send_hit.astype(jnp.int32), axis=1)
    send_index = jnp.where(
        occupied > 0, jnp.sum(jnp.where(send_hit, local_index[None, :], 0), axis=1), -1
    )
    recv_index = lax.all_to_all(send_index, "row", split_axis=0, concat_axis=0, tiled=True)
    recv_onehot = (recv_index[None, :] == jnp.arange(share_tiles, dtype=jnp.int32)[:, None]).astype(
        jnp.float32
    )
    cost_share = take_share(cost_vector)
    lower_share = take_share(lower_bound)
    width_share = take_share(bound_width)
    kind_share = take_share(variable_kind)

    def reduce_back(vector):
        sent = jnp.dot(send_onehot, backward_product(vector), precision=highest)
        arrived = lax.all_to_all(sent, "row", split_axis=0, concat_axis=0, tiled=True)
        return jnp.dot(recv_onehot, arrived, precision=highest).reshape(-1)

    primal = take_share(primal_start)
    image = forward_picked(primal_start[col_of])
    dual = dual_start
    step_size = step_start
    gradient = reduce_back(dual)
    for iteration in range(ITERS):
        primal_next = project_primal(
            primal - step_size / primal_weight * (cost_share - gradient),
            lower_share,
            width_share,
            kind_share,
        )
        back = jnp.dot(
            recv_onehot.T, primal_next.reshape(share_tiles, tile_width), precision=highest
        )
        returned = lax.all_to_all(back, "row", split_axis=0, concat_axis=0, tiled=True)
        image_next = forward_picked(jnp.dot(send_onehot.T, returned, precision=highest))
        dual_next = project_dual(
            dual + step_size * primal_weight * (right_side - 2.0 * image_next + image), row_kind
        )
        if iteration + 1 < ITERS:
            gradient = reduce_back(dual_next)
            change_dual = dual_next - dual
            change_primal = primal_next - primal
            cross_part = jnp.sum(change_dual * (image_next - image))
            dual_part = jnp.sum(change_dual * change_dual)
            primal_part = jnp.sum(change_primal * change_primal)
            cross, dual_square, primal_rows = lax.psum((cross_part, dual_part, primal_part), "row")
            primal_square = lax.psum(primal_rows, "col")
            step_size = next_step(
                cross, dual_square, primal_square, primal_weight, step_size, iteration
            )
        primal, dual, image = (primal_next, dual_next, image_next)
    primal = lax.all_gather(primal, "row", axis=0, tiled=True).reshape(col_tiles, tile_width)
    return (primal, dual)


def solution(mesh):
    return jax.shard_map(
        shards,
        mesh=mesh,
        in_specs=(
            P("row", "col", None, None, None),
            P("row", "col", None),
            P("col", None),
            P("col", None),
            P("col", None),
            P("col", None),
            P("row", None),
            P("row", None),
            P("col", None),
            P("row", None),
            P(),
            P(),
        ),
        out_specs=(P("col", None), P("row", None)),
        check_vma=False,
    )
```

profile of v0, /device:TPU:0, one launch (start us, length us, event | category | flops | bytes accessed | tf_op | source)
XLA Modules:
  0.0 292.4 jit_solution(2359915443829012869)
XLA Ops:
  0.6 0.7 and_select_fusion.1
  1.7 0.7 select_n.161
  2.4 7.3 %all-to-all-start = ((s32[8,2,1]{1,2,0:T(1,128)}), s32[8,2,1]{1,2,0:T(1,128)S(1)}, u32[]{:S(2)}, u32[]{:S(2)}) async-start(s32[8,2,1]{1,2,0:T(1,128)} %bitcast.1), calls=%async_computation | async-start | bytes 8192 | tf_op jit(solution)/shard_map/all_to_all | solution.py:82
  9.7 0.7 fusion.86
  10.3 1.3 gather_fusion
  11.7 4.3 %fusion.16 = f32[16,1,256]{2,1,0:T(1,128)S(1)} fusion(f32[1,1,16,256,256]{4,3,2,1,0:T(8,128)} %param.12, f32[16,256,1]{1,0,2:T(8,128)S(1)} %bitcast.156), kind=kOutput, calls=%fused_computation.21 | convolution fusion | flops 12582912 | bytes 4227072 | tf_op jit(solution)/shard_map/tij,ti->tj/dot_general | solution.py:60
  16.2 0.6 all_to_all.63
  16.8 0.6 gather_fusion.1
  17.4 6.0 %all-to-all-start.1 = ((f32[8,2,256]{2,1,0:T(2,128)}), f32[8,2,256]{2,1,0:T(2,128)S(1)}, u32[]{:S(2)}, u32[]{:S(2)}) async-start(f32[8,2,256]{2,1,0:T(2,128)} %all_to_all.63), calls=%async_computation.1 | async-start | bytes 32768 | tf_op jit(solution)/shard_map/all_to_all | solution.py:93
  23.4 5.7 %fusion.12 = f32[16,1,256]{2,1,0:T(1,128)S(1)} fusion(f32[1,1,16,256,256]{4,3,2,1,0:T(8,128)} %param.12, f32[16,256,1]{1,0,2:T(8,128)S(1)} %bitcast.154), kind=kOutput, calls=%fused_computation.17 | convolution fusion | flops 12582912 | bytes 4227072 | tf_op jit(solution)/shard_map/tij,tj->ti/dot_general | solution.py:54
  30.9 0.5 broadcast.428
  31.4 0.7 reduce.3
  32.4 0.6 multiply_reduce_fusion.8
  33.0 0.2 fusion.62
  33.2 0.6 copy.28
  33.8 6.0 %all-to-all-start.2 = ((f32[8,2,256]{2,1,0:T(2,128)}), f32[8,2,256]{2,1,0:T(2,128)S(1)}, u32[]{:S(2)}, u32[]{:S(2)}) async-start(f32[8,2,256]{2,1,0:T(2,128)} %copy.28), calls=%async_computation.2 | async-start | bytes 32768 | tf_op jit(solution)/shard_map/all_to_all | solution.py:111
  40.0 6.5 %all-to-all-done.2 = f32[8,2,256]{2,1,0:T(2,128)S(1)} async-done(((f32[8,2,256]{2,1,0:T(2,128)}), f32[8,2,256]{2,1,0:T(2,128)S(1)}, u32[]{:S(2)}, u32[]{:S(2)}) %all-to-all-start.2) | async-done | bytes 16416 | tf_op jit(solution)/shard_map/all_to_all | solution.py:111
  46.4 0.2 convolution_bitcast_fusion.6
  46.6 5.7 %fusion.14 = f32[16,1,256]{2,1,0:T(1,128)S(1)} fusion(f32[1,1,16,256,256]{4,3,2,1,0:T(8,128)} %param.12, f32[16,256,1]{1,0,2:T(8,128)S(1)} %convolution_bitcast_fusion.6), kind=kOutput, calls=%fused_computation.19 | convolution fusion | flops 12582912 | bytes 4227072 | tf_op jit(solution)/shard_map/tij,tj->ti/dot_general | solution.py:54
  52.4 10.5 %all-reduce.3 = (f32[16,256]{1,0:T(8,128)S(1)}, f32[16,256]{1,0:T(8,128)S(1)}) all-reduce(f32[16,256]{1,0:T(8,128)S(1)} %fusion.30, f32[16,256]{1,0:T(8,128)S(1)} %fusion.32), channel_id=1, replica_groups=mesh['row'=8,'col'=4] {'col'}, use_global_device_ids=true, to_apply=%region_7.8 | all-reduce | flops 8192 | bytes 65536 | tf_op jit(solution)/shard_map/psum | solution.py:56
  62.9 0.7 multiply_reduce_fusion.6
  63.6 0.6 gather_fusion.2
  64.2 4.3 %fusion.10 = f32[16,1,256]{2,1,0:T(1,128)S(1)} fusion(f32[1,1,16,256,256]{4,3,2,1,0:T(8,128)} %param.12, f32[16,256,1]{1,0,2:T(8,128)S(1)} %bitcast.157), kind=kOutput, calls=%fused_computation.15 | convolution fusion | flops 12582912 | bytes 4227072 | tf_op jit(solution)/shard_map/tij,ti->tj/dot_general | solution.py:60
  68.6 0.6 all_to_all.69
  69.3 3.3 %all-to-all-start.3 = ((f32[8,2,256]{2,1,0:T(2,128)}), f32[8,2,256]{2,1,0:T(2,128)S(1)}, u32[]{:S(2)}, u32[]{:S(2)}) async-start(f32[8,2,256]{2,1,0:T(2,128)} %all_to_all.69), calls=%async_computation.3 | async-start | bytes 32768 | tf_op jit(solution)/shard_map/all_to_all | solution.py:93
  72.6 22.5 %all-reduce.2 = (f32[]{:T(128)}, f32[]{:T(128)}, f32[]{:T(128)}) all-reduce(f32[]{:T(128)} %get-tuple-element.29, f32[]{:T(128)} %get-tuple-element.7, f32[]{:T(128)} %get-tuple-element.6), channel_id=1, replica_groups=mesh['row'=8,'col'=4] {'row'}, use_global_device_ids=true, to_apply=%region_4.5 | all-reduce | flops 3 | bytes 24 | tf_op jit(solution)/shard_map/psum | solution.py:123
  95.1 6.3 %psum.120 = f32[]{:T(128)} all-reduce(f32[]{:T(128)} %get-tuple-element.16), channel_id=1, replica_groups=mesh['row'=8,'col'=4] {'col'}, use_global_device_ids=true, to_apply=%region_5.6 | all-reduce | flops 1 | bytes 8 | tf_op jit(solution)/shard_map/psum | solution.py:124
  103.6 0.6 multiply_reduce_fusion.5
  104.2 0.2 fusion.60
  104.4 0.6 copy.29
  105.0 3.3 %all-to-all-start.4 = ((f32[8,2,256]{2,1,0:T(2,128)}), f32[8,2,256]{2,1,0:T(2,128)S(1)}, u32[]{:S(2)}, u32[]{:S(2)}) async-start(f32[8,2,256]{2,1,0:T(2,128)} %copy.29), calls=%async_computation.4 | async-start | bytes 32768 | tf_op jit(solution)/shard_map/all_to_all | solution.py:111
  108.4 6.5 %all-to-all-done.4 = f32[8,2,256]{2,1,0:T(2,128)S(1)} async-done(((f32[8,2,256]{2,1,0:T(2,128)}), f32[8,2,256]{2,1,0:T(2,128)S(1)}, u32[]{:S(2)}, u32[]{:S(2)}) %all-to-all-start.4) | async-done | bytes 16416 | tf_op jit(solution)/shard_map/all_to_all | solution.py:111
  114.9 0.2 convolution_bitcast_fusion.4
  115.1 5.7 %fusion.8 = f32[16,1,256]{2,1,0:T(1,128)S(1)} fusion(f32[1,1,16,256,256]{4,3,2,1,0:T(8,128)} %param.12, f32[16,256,1]{1,0,2:T(8,128)S(1)} %convolution_bitcast_fusion.4), kind=kOutput, calls=%fused_computation.13 | convolution fusion | flops 12582912 | bytes 4227072 | tf_op jit(solution)/shard_map/tij,tj->ti/dot_general | solution.py:54
  120.9 10.1 %psum.127 = f32[16,256]{1,0:T(8,128)S(1)} all-reduce(f32[16,256]{1,0:T(8,128)S(1)} %fusion.26), channel_id=1, replica_groups=mesh['row'=8,'col'=4] {'col'}, use_global_device_ids=true, to_apply=%region_15.16 | all-reduce | flops 4096 | bytes 32768 | tf_op jit(solution)/shard_map/psum | solution.py:56
  131.0 0.7 multiply_reduce_fusion.3
  131.7 0.6 gather_fusion.3
  132.3 4.3 %fusion.6 = f32[16,1,256]{2,1,0:T(1,128)S(1)} fusion(f32[1,1,16,256,256]{4,3,2,1,0:T(8,128)} %param.12, f32[16,256,1]{1,0,2:T(8,128)S(1)} %bitcast.158), kind=kOutput, calls=%fused_computation.11 | convolution fusion | flops 12582912 | bytes 4227072 | tf_op jit(solution)/shard_map/tij,ti->tj/dot_general | solution.py:60
  136.7 0.6 all_to_all.74
  137.3 3.3 %all-to-all-start.5 = ((f32[8,2,256]{2,1,0:T(2,128)}), f32[8,2,256]{2,1,0:T(2,128)S(1)}, u32[]{:S(2)}, u32[]{:S(2)}) async-start(f32[8,2,256]{2,1,0:T(2,128)} %all_to_all.74), calls=%async_computation.5 | async-start | bytes 32768 | tf_op jit(solution)/shard_map/all_to_all | solution.py:93
  140.7 22.5 %all-reduce.1 = (f32[]{:T(128)}, f32[]{:T(128)}, f32[]{:T(128)}) all-reduce(f32[]{:T(128)} %get-tuple-element.25, f32[]{:T(128)} %get-tuple-element.5, f32[]{:T(128)} %get-tuple-element.4), channel_id=1, replica_groups=mesh['row'=8,'col'=4] {'row'}, use_global_device_ids=true, to_apply=%region_13.14 | all-reduce | flops 3 | bytes 24 | tf_op jit(solution)/shard_map/psum | solution.py:123
  163.1 6.3 %psum.126 = f32[]{:T(128)} all-reduce(f32[]{:T(128)} %get-tuple-element.13), channel_id=1, replica_groups=mesh['row'=8,'col'=4] {'col'}, use_global_device_ids=true, to_apply=%region_14.15 | all-reduce | flops 1 | bytes 8 | tf_op jit(solution)/shard_map/psum | solution.py:124
  171.6 0.6 multiply_reduce_fusion.2
  172.4 0.6 copy.30
  173.1 3.6 %all-to-all-start.6 = ((f32[8,2,256]{2,1,0:T(2,128)}), f32[8,2,256]{2,1,0:T(2,128)S(1)}, u32[]{:S(2)}, u32[]{:S(2)}) async-start(f32[8,2,256]{2,1,0:T(2,128)} %copy.30), calls=%async_computation.6 | async-start | bytes 32768 | tf_op jit(solution)/shard_map/all_to_all | solution.py:111
  176.7 6.3 %all-to-all-done.6 = f32[8,2,256]{2,1,0:T(2,128)S(1)} async-done(((f32[8,2,256]{2,1,0:T(2,128)}), f32[8,2,256]{2,1,0:T(2,128)S(1)}, u32[]{:S(2)}, u32[]{:S(2)}) %all-to-all-start.6) | async-done | bytes 16416 | tf_op jit(solution)/shard_map/all_to_all | solution.py:111
  182.9 0.2 convolution_bitcast_fusion.2
  183.1 5.7 %fusion.4 = f32[16,1,256]{2,1,0:T(1,128)S(1)} fusion(f32[1,1,16,256,256]{4,3,2,1,0:T(8,128)} %param.12, f32[16,256,1]{1,0,2:T(8,128)S(1)} %convolution_bitcast_fusion.2), kind=kOutput, calls=%fused_computation.9 | convolution fusion | flops 12582912 | bytes 4227072 | tf_op jit(solution)/shard_map/tij,tj->ti/dot_general | solution.py:54
  188.9 10.1 %psum.132 = f32[16,256]{1,0:T(8,128)S(1)} all-reduce(f32[16,256]{1,0:T(8,128)S(1)} %fusion.22), channel_id=1, replica_groups=mesh['row'=8,'col'=4] {'col'}, use_global_device_ids=true, to_apply=%region_23.24 | all-reduce | flops 4096 | bytes 32768 | tf_op jit(solution)/shard_map/psum | solution.py:56
  199.1 0.7 multiply_reduce_fusion
  199.7 0.6 gather_fusion.4
  200.3 4.3 %fusion.2 = f32[16,1,256]{2,1,0:T(1,128)S(1)} fusion(f32[1,1,16,256,256]{4,3,2,1,0:T(8,128)} %param.12, f32[16,256,1]{1,0,2:T(8,128)S(1)} %bitcast.155), kind=kOutput, calls=%fused_computation.7 | convolution fusion | flops 12582912 | bytes 4227072 | tf_op jit(solution)/shard_map/tij,ti->tj/dot_general | solution.py:60
  204.7 0.6 all_to_all.79
  205.4 3.3 %all-to-all-start.7 = ((f32[8,2,256]{2,1,0:T(2,128)}), f32[8,2,256]{2,1,0:T(2,128)S(1)}, u32[]{:S(2)}, u32[]{:S(2)}) async-start(f32[8,2,256]{2,1,0:T(2,128)} %all_to_all.79), calls=%async_computation.7 | async-start | bytes 32768 | tf_op jit(solution)/shard_map/all_to_all | solution.py:93
  208.7 22.5 %all-reduce = (f32[]{:T(128)}, f32[]{:T(128)}, f32[]{:T(128)}) all-reduce(f32[]{:T(128)} %get-tuple-element.22, f32[]{:T(128)} %get-tuple-element.3, f32[]{:T(128)} %get-tuple-element.2), channel_id=1, replica_groups=mesh['row'=8,'col'=4] {'row'}, use_global_device_ids=true, to_apply=%region_21.22 | all-reduce | flops 3 | bytes 24 | tf_op jit(solution)/shard_map/psum | solution.py:123
  231.2 6.3 %psum.131 = f32[]{:T(128)} all-reduce(f32[]{:T(128)} %get-tuple-element.10), channel_id=1, replica_groups=mesh['row'=8,'col'=4] {'col'}, use_global_device_ids=true, to_apply=%region_22.23 | all-reduce | flops 1 | bytes 8 | tf_op jit(solution)/shard_map/psum | solution.py:124
  239.9 0.6 copy.31
  240.6 3.3 %all-to-all-start.8 = ((f32[8,2,256]{2,1,0:T(2,128)}), f32[8,2,256]{2,1,0:T(2,128)S(1)}, u32[]{:S(2)}, u32[]{:S(2)}) async-start(f32[8,2,256]{2,1,0:T(2,128)} %copy.31), calls=%async_computation.8 | async-start | bytes 32768 | tf_op jit(solution)/shard_map/all_to_all | solution.py:111
  243.9 31.0 %all_gather.3 = f32[32768]{0:T(1024)S(1)} all-gather(f32[4096]{0:T(1024)S(1)} %minimum_select_fusion), channel_id=1, replica_groups=mesh['row'=8,'col'=4] {'row'}, dimensions={0}, use_global_device_ids=true | all-gather | bytes 147456 | tf_op jit(solution)/shard_map/all_gather | solution.py:129
  274.9 0.7 reshape.368
  275.6 0.2 convolution_bitcast_fusion
  275.8 5.7 %fusion = f32[16,1,256]{2,1,0:T(1,128)S(1)} fusion(f32[1,1,16,256,256]{4,3,2,1,0:T(8,128)} %param.12, f32[16,256,1]{1,0,2:T(8,128)S(1)} %convolution_bitcast_fusion), kind=kOutput, calls=%fused_computation.5 | convolution fusion | flops 12582912 | bytes 4227072 | tf_op jit(solution)/shard_map/tij,tj->ti/dot_general | solution.py:54
  281.6 10.1 %psum.135 = f32[16,256]{1,0:T(8,128)S(1)} all-reduce(f32[16,256]{1,0:T(8,128)S(1)} %fusion.18), channel_id=1, replica_groups=mesh['row'=8,'col'=4] {'col'}, use_global_device_ids=true, to_apply=%region_28.29 | all-reduce | flops 4096 | bytes 32768 | tf_op jit(solution)/shard_map/psum | solution.py:56
  291.7 0.6 maximum_select_fusion
  (68 shorter events, 3.2 us)
Async XLA Ops:
  0.6 16.2 %copy-start.1 = (f32[128,256]{1,0:T(8,128)S(1)}, f32[128,256]{1,0:T(8,128)}, u32[]{:S(2)}) copy-start(f32[128,256]{1,0:T(8,128)} %param.20) | copy-start | bytes 393220
  2.4 15.0 %all-to-all-start = ((s32[8,2,1]{1,2,0:T(1,128)}), s32[8,2,1]{1,2,0:T(1,128)S(1)}, u32[]{:S(2)}, u32[]{:S(2)}) async-start(s32[8,2,1]{1,2,0:T(1,128)} %bitcast.1), calls=%async_computation | async-start | bytes 8192 | tf_op jit(solution)/shard_map/all_to_all | solution.py:82
  11.6 18.8 %copy-start.3 = (f32[128,256]{1,0:T(8,128)S(1)}, f32[128,256]{1,0:T(8,128)}, u32[]{:S(2)}) copy-start(f32[128,256]{1,0:T(8,128)} %param.14) | copy-start | bytes 393220
  11.7 18.9 %copy-start.4 = (f32[128,256]{1,0:T(8,128)S(1)}, f32[128,256]{1,0:T(8,128)}, u32[]{:S(2)}) copy-start(f32[128,256]{1,0:T(8,128)} %param.15) | copy-start | bytes 393220
  11.7 18.9 %copy-start.5 = (f32[128,256]{1,0:T(8,128)S(1)}, f32[128,256]{1,0:T(8,128)}, u32[]{:S(2)}) copy-start(f32[128,256]{1,0:T(8,128)} %param.16) | copy-start | bytes 393220
  11.7 19.0 %copy-start.6 = (s32[128,256]{1,0:T(8,128)S(1)}, s32[128,256]{1,0:T(8,128)}, u32[]{:S(2)}) copy-start(s32[128,256]{1,0:T(8,128)} %param.17) | copy-start | bytes 393220
  17.4 14.8 %all-to-all-start.1 = ((f32[8,2,256]{2,1,0:T(2,128)}), f32[8,2,256]{2,1,0:T(2,128)S(1)}, u32[]{:S(2)}, u32[]{:S(2)}) async-start(f32[8,2,256]{2,1,0:T(2,128)} %all_to_all.63), calls=%async_computation.1 | async-start | bytes 32768 | tf_op jit(solution)/shard_map/all_to_all | solution.py:93
  23.4 39.5 %copy-start = (f32[16,256]{1,0:T(8,128)S(1)}, f32[16,256]{1,0:T(8,128)}, u32[]{:S(2)}) copy-start(f32[16,256]{1,0:T(8,128)} %param.21) | copy-start | bytes 49156
  23.4 39.5 %copy-start.2 = (f32[16,256]{1,0:T(8,128)S(1)}, f32[16,256]{1,0:T(8,128)}, u32[]{:S(2)}) copy-start(f32[16,256]{1,0:T(8,128)} %param.18) | copy-start | bytes 49156
  23.4 39.5 %copy-start.7 = (s32[16,256]{1,0:T(8,128)S(1)}, s32[16,256]{1,0:T(8,128)}, u32[]{:S(2)}) copy-start(s32[16,256]{1,0:T(8,128)} %param.19) | copy-start | bytes 49156
  33.8 12.6 %all-to-all-start.2 = ((f32[8,2,256]{2,1,0:T(2,128)}), f32[8,2,256]{2,1,0:T(2,128)S(1)}, u32[]{:S(2)}, u32[]{:S(2)}) async-start(f32[8,2,256]{2,1,0:T(2,128)} %copy.28), calls=%async_computation.2 | async-start | bytes 32768 | tf_op jit(solution)/shard_map/all_to_all | solution.py:111
  69.3 34.1 %all-to-all-start.3 = ((f32[8,2,256]{2,1,0:T(2,128)}), f32[8,2,256]{2,1,0:T(2,128)S(1)}, u32[]{:S(2)}, u32[]{:S(2)}) async-start(f32[8,2,256]{2,1,0:T(2,128)} %all_to_all.69), calls=%async_computation.3 | async-start | bytes 32768 | tf_op jit(solution)/shard_map/all_to_all | solution.py:93
  105.0 9.9 %all-to-all-start.4 = ((f32[8,2,256]{2,1,0:T(2,128)}), f32[8,2,256]{2,1,0:T(2,128)S(1)}, u32[]{:S(2)}, u32[]{:S(2)}) async-start(f32[8,2,256]{2,1,0:T(2,128)} %copy.29), calls=%async_computation.4 | async-start | bytes 32768 | tf_op jit(solution)/shard_map/all_to_all | solution.py:111
  137.3 34.1 %all-to-all-start.5 = ((f32[8,2,256]{2,1,0:T(2,128)}), f32[8,2,256]{2,1,0:T(2,128)S(1)}, u32[]{:S(2)}, u32[]{:S(2)}) async-start(f32[8,2,256]{2,1,0:T(2,128)} %all_to_all.74), calls=%async_computation.5 | async-start | bytes 32768 | tf_op jit(solution)/shard_map/all_to_all | solution.py:93
  173.1 9.9 %all-to-all-start.6 = ((f32[8,2,256]{2,1,0:T(2,128)}), f32[8,2,256]{2,1,0:T(2,128)S(1)}, u32[]{:S(2)}, u32[]{:S(2)}) async-start(f32[8,2,256]{2,1,0:T(2,128)} %copy.30), calls=%async_computation.6 | async-start | bytes 32768 | tf_op jit(solution)/shard_map/all_to_all | solution.py:111
  205.4 34.2 %all-to-all-start.7 = ((f32[8,2,256]{2,1,0:T(2,128)}), f32[8,2,256]{2,1,0:T(2,128)S(1)}, u32[]{:S(2)}, u32[]{:S(2)}) async-start(f32[8,2,256]{2,1,0:T(2,128)} %all_to_all.79), calls=%async_computation.7 | async-start | bytes 32768 | tf_op jit(solution)/shard_map/all_to_all | solution.py:93
  240.6 35.0 %all-to-all-start.8 = ((f32[8,2,256]{2,1,0:T(2,128)}), f32[8,2,256]{2,1,0:T(2,128)S(1)}, u32[]{:S(2)}, u32[]{:S(2)}) async-start(f32[8,2,256]{2,1,0:T(2,128)} %copy.31), calls=%async_computation.8 | async-start | bytes 32768 | tf_op jit(solution)/shard_map/all_to_all | solution.py:111
where the time goes:
time: 294 us; the launch traced here: 292 us
  blocking collectives  158 us (54%)
  matrix products  48.7 us (17%)
  starting transfers between devices  39.6 us (13%)
  waiting for transfers between devices  19.2 us (7%)
  local copies, waits for them, and re-layouts  11.3 us (4%)
  between operations  8.64 us (3%)
  other arithmetic  6.96 us (2%)
    psum x3, blocking collectives, shards(): lax.psum((cross_part, dual_part, primal_part), 'row')  67.4 us
    psum x4, blocking collectives, forward_picked(): return lax.psum(partial_rows, 'col')  40.9 us
    all_gather x1, blocking collectives, shards(): lax.all_gather(primal, 'row', axis=0, tiled=True)  31 us
    dot_general x5, matrix products, forward_picked(): product = jnp.einsum('tij,tj->ti', tile_set, picked, precision=highest)  28.3 us
    all_to_all x4, waiting for transfers between devices, shards(): lax.all_to_all(back, 'row', split_axis=0, concat_axis=0, tiled=True)  19.2 us
    psum x3, blocking collectives, shards(): primal_square = lax.psum(primal_rows, 'col')  18.8 us
    dot_general x4, matrix products, backward_product(): return jnp.einsum('tij,ti->tj', tile_set, picked, precision=highest)  17.2 us
    all_to_all x4, starting transfers between devices, shards(): lax.all_to_all(back, 'row', split_axis=0, concat_axis=0, tiled=True)  16.2 us
  transfers between devices with their start and end apart: 9, of which 3 were waited for; matrix products, arithmetic and copies ran while one was open for 5% of the time, Pallas kernels for 0%

commit v1 on v0

--- a/solution.py
+++ b/solution.py
@@ -5,6 +5,12 @@
 
 ITERS = 4
 highest = lax.Precision.HIGHEST
+
+
+def summed_here(x, mesh_axis):
+    blocks = lax.all_gather(x, mesh_axis, axis=0, tiled=False)
+    total = blocks.sum(axis=0)
+    return total
 
 
 def project_primal(values, lower_bound, bound_width, variable_kind):
@@ -53,7 +59,7 @@
     def forward_picked(picked):
         product = jnp.einsum("tij,tj->ti", tile_set, picked, precision=highest)
         partial_rows = jnp.dot(row_onehot, product, precision=highest)
-        return lax.psum(partial_rows, "col")
+        return summed_here(partial_rows, "col")
 
     def backward_product(vector):
         picked = vector[row_of]

time: 294 us -> 276 us (0.939)
  blocking collectives: 158 us -> 144 us
  waiting for transfers between devices: 19.2 us -> 13.9 us
    psum x4 -> x0, blocking collectives: 40.9 us -> none  [forward_picked(): return lax.psum(partial_rows, 'col')]
    all_gather x0 -> x5, blocking collectives: none -> 26.4 us  [summed_here(): blocks = lax.all_gather(x, mesh_axis, axis=0, tiled=False)]
    all_to_all x4, waiting for transfers between devices: 19.2 us -> 13.9 us  [shards(): lax.all_to_all(back, 'row', split_axis=0, concat_axis=0, tiled=True)]
  transfers between devices with their start and end apart: 9 -> 9, of which waited for: 3 -> 3; matrix products, arithmetic and copies ran while one was open for 5% -> 6% of each run, Pallas kernels for 0% -> 0%
where the time goes in v1:
time: 276 us; the launch traced here: 274 us
  blocking collectives  144 us (52%)
  matrix products  48.7 us (18%)
  starting transfers between devices  41 us (15%)
  waiting for transfers between devices  13.9 us (5%)
  local copies, waits for them, and re-layouts  11.3 us (4%)
  between operations  8.62 us (3%)
  other arithmetic  6.99 us (3%)
    psum x3, blocking collectives, shards(): lax.psum((cross_part, dual_part, primal_part), 'row')  67.5 us
    all_gather x1, blocking collectives, shards(): lax.all_gather(primal, 'row', axis=0, tiled=True)  31 us
    dot_general x5, matrix products, forward_picked(): product = jnp.einsum('tij,tj->ti', tile_set, picked, precision=highest)  28.3 us
    all_gather x5, blocking collectives, summed_here(): blocks = lax.all_gather(x, mesh_axis, axis=0, tiled=False)  26.4 us
    psum x3, blocking collectives, shards(): primal_square = lax.psum(primal_rows, 'col')  18.8 us
    all_to_all x4, starting transfers between devices, reduce_back(): lax.all_to_all(sent, 'row', split_axis=0, concat_axis=0, tiled=True)  17.5 us
    dot_general x4, matrix products, backward_product(): return jnp.einsum('tij,ti->tj', tile_set, picked, precision=highest)  17.2 us
    all_to_all x4, starting transfers between devices, shards(): lax.all_to_all(back, 'row', split_axis=0, concat_axis=0, tiled=True)  16.2 us
  transfers between devices with their start and end apart: 9, of which 3 were waited for; matrix products, arithmetic and copies ran while one was open for 6% of the time, Pallas kernels for 0%

profile of v1, /device:TPU:0, one launch (start us, length us, event | category | flops | bytes accessed | tf_op | source)
XLA Modules:
  0.0 274.2 jit_solution(14328628505180261410)
XLA Ops:
  0.6 0.7 and_select_fusion.1
  1.7 0.7 select_n.161
  2.4 7.3 %all-to-all-start = ((s32[8,2,1]{1,2,0:T(1,128)}), s32[8,2,1]{1,2,0:T(1,128)S(1)}, u32[]{:S(2)}, u32[]{:S(2)}) async-start(s32[8,2,1]{1,2,0:T(1,128)} %bitcast.1), calls=%async_computation | async-start | bytes 8192 | tf_op jit(solution)/shard_map/all_to_all | solution.py:88
  9.7 0.7 fusion.86
  10.3 1.3 gather_fusion
  11.7 4.3 %fusion.16 = f32[16,1,256]{2,1,0:T(1,128)S(1)} fusion(f32[1,1,16,256,256]{4,3,2,1,0:T(8,128)} %param.12, f32[16,256,1]{1,0,2:T(8,128)S(1)} %bitcast.166), kind=kOutput, calls=%fused_computation.21 | convolution fusion | flops 12582912 | bytes 4227072 | tf_op jit(solution)/shard_map/tij,ti->tj/dot_general | solution.py:66
  16.2 0.6 all_to_all.63
  16.8 0.6 gather_fusion.1
  17.4 6.0 %all-to-all-start.1 = ((f32[8,2,256]{2,1,0:T(2,128)}), f32[8,2,256]{2,1,0:T(2,128)S(1)}, u32[]{:S(2)}, u32[]{:S(2)}) async-start(f32[8,2,256]{2,1,0:T(2,128)} %all_to_all.63), calls=%async_computation.1 | async-start | bytes 32768 | tf_op jit(solution)/shard_map/all_to_all | solution.py:99
  23.4 5.7 %fusion.12 = f32[16,1,256]{2,1,0:T(1,128)S(1)} fusion(f32[1,1,16,256,256]{4,3,2,1,0:T(8,128)} %param.12, f32[16,256,1]{1,0,2:T(8,128)S(1)} %bitcast.164), kind=kOutput, calls=%fused_computation.17 | convolution fusion | flops 12582912 | bytes 4227072 | tf_op jit(solution)/shard_map/tij,tj->ti/dot_general | solution.py:60
  30.9 0.5 broadcast.428
  31.4 0.7 reduce.3
  32.4 0.6 multiply_reduce_fusion.8
  33.0 0.2 fusion.62
  33.2 0.6 copy.28
  33.8 6.0 %all-to-all-start.2 = ((f32[8,2,256]{2,1,0:T(2,128)}), f32[8,2,256]{2,1,0:T(2,128)S(1)}, u32[]{:S(2)}, u32[]{:S(2)}) async-start(f32[8,2,256]{2,1,0:T(2,128)} %copy.28), calls=%async_computation.2 | async-start | bytes 32768 | tf_op jit(solution)/shard_map/all_to_all | solution.py:117
  40.0 5.2 %all-gather.1 = f32[64,256]{1,0:T(8,128)S(1)} all-gather(f32[16,256]{1,0:T(8,128)S(1)} %fusion.30), channel_id=3, replica_groups=mesh['row'=8,'col'=4] {'col'}, dimensions={0}, use_global_device_ids=true | all-gather | bytes 81920 | tf_op jit(solution)/shard_map/all_gather | solution.py:11
  45.2 1.2 all-to-all-done.2
  46.4 0.2 convolution_bitcast_fusion.6
  46.6 5.7 %fusion.14 = f32[16,1,256]{2,1,0:T(1,128)S(1)} fusion(f32[1,1,16,256,256]{4,3,2,1,0:T(8,128)} %param.12, f32[16,256,1]{1,0,2:T(8,128)S(1)} %convolution_bitcast_fusion.6), kind=kOutput, calls=%fused_computation.19 | convolution fusion | flops 12582912 | bytes 4227072 | tf_op jit(solution)/shard_map/tij,tj->ti/dot_general | solution.py:60
  52.4 5.4 %all-gather = f32[64,256]{1,0:T(8,128)S(1)} all-gather(f32[16,256]{1,0:T(8,128)S(1)} %fusion.32), channel_id=2, replica_groups=mesh['row'=8,'col'=4] {'col'}, dimensions={0}, use_global_device_ids=true | all-gather | bytes 81920 | tf_op jit(solution)/shard_map/all_gather | solution.py:11
  57.9 0.7 multiply_reduce_fusion.6
  58.6 0.6 gather_fusion.2
  59.1 4.3 %fusion.10 = f32[16,1,256]{2,1,0:T(1,128)S(1)} fusion(f32[1,1,16,256,256]{4,3,2,1,0:T(8,128)} %param.12, f32[16,256,1]{1,0,2:T(8,128)S(1)} %bitcast.167), kind=kOutput, calls=%fused_computation.15 | convolution fusion | flops 12582912 | bytes 4227072 | tf_op jit(solution)/shard_map/tij,ti->tj/dot_general | solution.py:66
  63.5 0.6 all_to_all.69
  64.2 4.8 %all-to-all-start.3 = ((f32[8,2,256]{2,1,0:T(2,128)}), f32[8,2,256]{2,1,0:T(2,128)S(1)}, u32[]{:S(2)}, u32[]{:S(2)}) async-start(f32[8,2,256]{2,1,0:T(2,128)} %all_to_all.69), calls=%async_computation.3 | async-start | bytes 32768 | tf_op jit(solution)/shard_map/all_to_all | solution.py:99
  69.0 22.5 %all-reduce.2 = (f32[]{:T(128)}, f32[]{:T(128)}, f32[]{:T(128)}) all-reduce(f32[]{:T(128)} %get-tuple-element.27, f32[]{:T(128)} %get-tuple-element.7, f32[]{:T(128)} %get-tuple-element.6), channel_id=1, replica_groups=mesh['row'=8,'col'=4] {'row'}, use_global_device_ids=true, to_apply=%region_4.5 | all-reduce | flops 3 | bytes 24 | tf_op jit(solution)/shard_map/psum | solution.py:129
  91.5 6.3 %psum.85 = f32[]{:T(128)} all-reduce(f32[]{:T(128)} %get-tuple-element.16), channel_id=1, replica_groups=mesh['row'=8,'col'=4] {'col'}, use_global_device_ids=true, to_apply=%region_5.6 | all-reduce | flops 1 | bytes 8 | tf_op jit(solution)/shard_map/psum | solution.py:130
  100.0 0.6 multiply_reduce_fusion.5
  100.8 0.6 copy.29
  101.5 3.3 %all-to-all-start.4 = ((f32[8,2,256]{2,1,0:T(2,128)}), f32[8,2,256]{2,1,0:T(2,128)S(1)}, u32[]{:S(2)}, u32[]{:S(2)}) async-start(f32[8,2,256]{2,1,0:T(2,128)} %copy.29), calls=%async_computation.4 | async-start | bytes 32768 | tf_op jit(solution)/shard_map/all_to_all | solution.py:117
  104.8 6.5 %all-to-all-done.4 = f32[8,2,256]{2,1,0:T(2,128)S(1)} async-done(((f32[8,2,256]{2,1,0:T(2,128)}), f32[8,2,256]{2,1,0:T(2,128)S(1)}, u32[]{:S(2)}, u32[]{:S(2)}) %all-to-all-start.4) | async-done | bytes 16416 | tf_op jit(solution)/shard_map/all_to_all | solution.py:117
  111.3 0.2 convolution_bitcast_fusion.4
  111.5 5.7 %fusion.8 = f32[16,1,256]{2,1,0:T(1,128)S(1)} fusion(f32[1,1,16,256,256]{4,3,2,1,0:T(8,128)} %param.12, f32[16,256,1]{1,0,2:T(8,128)S(1)} %convolution_bitcast_fusion.4), kind=kOutput, calls=%fused_computation.13 | convolution fusion | flops 12582912 | bytes 4227072 | tf_op jit(solution)/shard_map/tij,tj->ti/dot_general | solution.py:60
  117.3 5.2 %all-gather.2 = f32[64,256]{1,0:T(8,128)S(1)} all-gather(f32[16,256]{1,0:T(8,128)S(1)} %fusion.26), channel_id=4, replica_groups=mesh['row'=8,'col'=4] {'col'}, dimensions={0}, use_global_device_ids=true | all-gather | bytes 81920 | tf_op jit(solution)/shard_map/all_gather | solution.py:11
  122.6 0.7 multiply_reduce_fusion.3
  123.3 0.6 gather_fusion.3
  123.8 4.3 %fusion.6 = f32[16,1,256]{2,1,0:T(1,128)S(1)} fusion(f32[1,1,16,256,256]{4,3,2,1,0:T(8,128)} %param.12, f32[16,256,1]{1,0,2:T(8,128)S(1)} %bitcast.168), kind=kOutput, calls=%fused_computation.11 | convolution fusion | flops 12582912 | bytes 4227072 | tf_op jit(solution)/shard_map/tij,ti->tj/dot_general | solution.py:66
  128.2 0.6 all_to_all.74
  128.9 3.3 %all-to-all-start.5 = ((f32[8,2,256]{2,1,0:T(2,128)}), f32[8,2,256]{2,1,0:T(2,128)S(1)}, u32[]{:S(2)}, u32[]{:S(2)}) async-start(f32[8,2,256]{2,1,0:T(2,128)} %all_to_all.74), calls=%async_computation.5 | async-start | bytes 32768 | tf_op jit(solution)/shard_map/all_to_all | solution.py:99
  132.2 22.5 %all-reduce.1 = (f32[]{:T(128)}, f32[]{:T(128)}, f32[]{:T(128)}) all-reduce(f32[]{:T(128)} %get-tuple-element.23, f32[]{:T(128)} %get-tuple-element.5, f32[]{:T(128)} %get-tuple-element.4), channel_id=1, replica_groups=mesh['row'=8,'col'=4] {'row'}, use_global_device_ids=true, to_apply=%region_13.14 | all-reduce | flops 3 | bytes 24 | tf_op jit(solution)/shard_map/psum | solution.py:129
  154.7 6.3 %psum.89 = f32[]{:T(128)} all-reduce(f32[]{:T(128)} %get-tuple-element.13), channel_id=1, replica_groups=mesh['row'=8,'col'=4] {'col'}, use_global_device_ids=true, to_apply=%region_14.15 | all-reduce | flops 1 | bytes 8 | tf_op jit(solution)/shard_map/psum | solution.py:130
  163.2 0.6 multiply_reduce_fusion.2
  164.0 0.6 copy.30
  164.6 3.6 %all-to-all-start.6 = ((f32[8,2,256]{2,1,0:T(2,128)}), f32[8,2,256]{2,1,0:T(2,128)S(1)}, u32[]{:S(2)}, u32[]{:S(2)}) async-start(f32[8,2,256]{2,1,0:T(2,128)} %copy.30), calls=%async_computation.6 | async-start | bytes 32768 | tf_op jit(solution)/shard_map/all_to_all | solution.py:117
  168.2 6.3 %all-to-all-done.6 = f32[8,2,256]{2,1,0:T(2,128)S(1)} async-done(((f32[8,2,256]{2,1,0:T(2,128)}), f32[8,2,256]{2,1,0:T(2,128)S(1)}, u32[]{:S(2)}, u32[]{:S(2)}) %all-to-all-start.6) | async-done | bytes 16416 | tf_op jit(solution)/shard_map/all_to_all | solution.py:117
  174.5 0.2 convolution_bitcast_fusion.2
  174.7 5.7 %fusion.4 = f32[16,1,256]{2,1,0:T(1,128)S(1)} fusion(f32[1,1,16,256,256]{4,3,2,1,0:T(8,128)} %param.12, f32[16,256,1]{1,0,2:T(8,128)S(1)} %convolution_bitcast_fusion.2), kind=kOutput, calls=%fused_computation.9 | convolution fusion | flops 12582912 | bytes 4227072 | tf_op jit(solution)/shard_map/tij,tj->ti/dot_general | solution.py:60
  180.5 5.2 %all-gather.3 = f32[64,256]{1,0:T(8,128)S(1)} all-gather(f32[16,256]{1,0:T(8,128)S(1)} %fusion.22), channel_id=5, replica_groups=mesh['row'=8,'col'=4] {'col'}, dimensions={0}, use_global_device_ids=true | all-gather | bytes 81920 | tf_op jit(solution)/shard_map/all_gather | solution.py:11
  185.7 0.7 multiply_reduce_fusion
  186.4 0.6 gather_fusion.4
  187.0 4.3 %fusion.2 = f32[16,1,256]{2,1,0:T(1,128)S(1)} fusion(f32[1,1,16,256,256]{4,3,2,1,0:T(8,128)} %param.12, f32[16,256,1]{1,0,2:T(8,128)S(1)} %bitcast.165), kind=kOutput, calls=%fused_computation.7 | convolution fusion | flops 12582912 | bytes 4227072 | tf_op jit(solution)/shard_map/tij,ti->tj/dot_general | solution.py:66
  191.4 0.6 all_to_all.79
  192.0 3.3 %all-to-all-start.7 = ((f32[8,2,256]{2,1,0:T(2,128)}), f32[8,2,256]{2,1,0:T(2,128)S(1)}, u32[]{:S(2)}, u32[]{:S(2)}) async-start(f32[8,2,256]{2,1,0:T(2,128)} %all_to_all.79), calls=%async_computation.7 | async-start | bytes 32768 | tf_op jit(solution)/shard_map/all_to_all | solution.py:99
  195.4 22.5 %all-reduce = (f32[]{:T(128)}, f32[]{:T(128)}, f32[]{:T(128)}) all-reduce(f32[]{:T(128)} %get-tuple-element.20, f32[]{:T(128)} %get-tuple-element.3, f32[]{:T(128)} %get-tuple-element.2), channel_id=1, replica_groups=mesh['row'=8,'col'=4] {'row'}, use_global_device_ids=true, to_apply=%region_21.22 | all-reduce | flops 3 | bytes 24 | tf_op jit(solution)/shard_map/psum | solution.py:129
  217.9 6.3 %psum.93 = f32[]{:T(128)} all-reduce(f32[]{:T(128)} %get-tuple-element.10), channel_id=1, replica_groups=mesh['row'=8,'col'=4] {'col'}, use_global_device_ids=true, to_apply=%region_22.23 | all-reduce | flops 1 | bytes 8 | tf_op jit(solution)/shard_map/psum | solution.py:130
  226.6 0.6 copy.31
  227.3 3.3 %all-to-all-start.8 = ((f32[8,2,256]{2,1,0:T(2,128)}), f32[8,2,256]{2,1,0:T(2,128)S(1)}, u32[]{:S(2)}, u32[]{:S(2)}) async-start(f32[8,2,256]{2,1,0:T(2,128)} %copy.31), calls=%async_computation.8 | async-start | bytes 32768 | tf_op jit(solution)/shard_map/all_to_all | solution.py:117
  230.6 31.0 %all_gather.41 = f32[32768]{0:T(1024)S(1)} all-gather(f32[4096]{0:T(1024)S(1)} %minimum_select_fusion), channel_id=1, replica_groups=mesh['row'=8,'col'=4] {'row'}, dimensions={0}, use_global_device_ids=true | all-gather | bytes 147456 | tf_op jit(solution)/shard_map/all_gather | solution.py:135
  261.6 0.7 reshape.368
  262.3 0.2 convolution_bitcast_fusion
  262.5 5.7 %fusion = f32[16,1,256]{2,1,0:T(1,128)S(1)} fusion(f32[1,1,16,256,256]{4,3,2,1,0:T(8,128)} %param.12, f32[16,256,1]{1,0,2:T(8,128)S(1)} %convolution_bitcast_fusion), kind=kOutput, calls=%fused_computation.5 | convolution fusion | flops 12582912 | bytes 4227072 | tf_op jit(solution)/shard_map/tij,tj->ti/dot_general | solution.py:60
  268.3 5.2 %all-gather.4 = f32[64,256]{1,0:T(8,128)S(1)} all-gather(f32[16,256]{1,0:T(8,128)S(1)} %fusion.18), channel_id=6, replica_groups=mesh['row'=8,'col'=4] {'col'}, dimensions={0}, use_global_device_ids=true | all-gather | bytes 81920 | tf_op jit(solution)/shard_map/all_gather | solution.py:11
  273.5 0.6 maximum_select_fusion
  (74 shorter events, 3.4 us)
Async XLA Ops:
  0.6 16.2 %copy-start.1 = (f32[128,256]{1,0:T(8,128)S(1)}, f32[128,256]{1,0:T(8,128)}, u32[]{:S(2)}) copy-start(f32[128,256]{1,0:T(8,128)} %param.20) | copy-start | bytes 393220
  2.4 15.0 %all-to-all-start = ((s32[8,2,1]{1,2,0:T(1,128)}), s32[8,2,1]{1,2,0:T(1,128)S(1)}, u32[]{:S(2)}, u32[]{:S(2)}) async-start(s32[8,2,1]{1,2,0:T(1,128)} %bitcast.1), calls=%async_computation | async-start | bytes 8192 | tf_op jit(solution)/shard_map/all_to_all | solution.py:88
  11.6 18.8 %copy-start.3 = (f32[128,256]{1,0:T(8,128)S(1)}, f32[128,256]{1,0:T(8,128)}, u32[]{:S(2)}) copy-start(f32[128,256]{1,0:T(8,128)} %param.14) | copy-start | bytes 393220
  11.7 18.8 %copy-start.4 = (f32[128,256]{1,0:T(8,128)S(1)}, f32[128,256]{1,0:T(8,128)}, u32[]{:S(2)}) copy-start(f32[128,256]{1,0:T(8,128)} %param.15) | copy-start | bytes 393220
  11.7 18.9 %copy-start.5 = (f32[128,256]{1,0:T(8,128)S(1)}, f32[128,256]{1,0:T(8,128)}, u32[]{:S(2)}) copy-start(f32[128,256]{1,0:T(8,128)} %param.16) | copy-start | bytes 393220
  11.7 19.0 %copy-start.6 = (s32[128,256]{1,0:T(8,128)S(1)}, s32[128,256]{1,0:T(8,128)}, u32[]{:S(2)}) copy-start(s32[128,256]{1,0:T(8,128)} %param.17) | copy-start | bytes 393220
  17.4 14.8 %all-to-all-start.1 = ((f32[8,2,256]{2,1,0:T(2,128)}), f32[8,2,256]{2,1,0:T(2,128)S(1)}, u32[]{:S(2)}, u32[]{:S(2)}) async-start(f32[8,2,256]{2,1,0:T(2,128)} %all_to_all.63), calls=%async_computation.1 | async-start | bytes 32768 | tf_op jit(solution)/shard_map/all_to_all | solution.py:99
  29.1 28.8 %copy-start = (f32[16,256]{1,0:T(8,128)S(1)}, f32[16,256]{1,0:T(8,128)}, u32[]{:S(2)}) copy-start(f32[16,256]{1,0:T(8,128)} %param.21) | copy-start | bytes 49156
  29.1 28.8 %copy-start.2 = (f32[16,256]{1,0:T(8,128)S(1)}, f32[16,256]{1,0:T(8,128)}, u32[]{:S(2)}) copy-start(f32[16,256]{1,0:T(8,128)} %param.18) | copy-start | bytes 49156
  29.1 28.8 %copy-start.7 = (s32[16,256]{1,0:T(8,128)S(1)}, s32[16,256]{1,0:T(8,128)}, u32[]{:S(2)}) copy-start(s32[16,256]{1,0:T(8,128)} %param.19) | copy-start | bytes 49156
  33.8 12.6 %all-to-all-start.2 = ((f32[8,2,256]{2,1,0:T(2,128)}), f32[8,2,256]{2,1,0:T(2,128)S(1)}, u32[]{:S(2)}, u32[]{:S(2)}) async-start(f32[8,2,256]{2,1,0:T(2,128)} %copy.28), calls=%async_computation.2 | async-start | bytes 32768 | tf_op jit(solution)/shard_map/all_to_all | solution.py:117
  64.2 35.6 %all-to-all-start.3 = ((f32[8,2,256]{2,1,0:T(2,128)}), f32[8,2,256]{2,1,0:T(2,128)S(1)}, u32[]{:S(2)}, u32[]{:S(2)}) async-start(f32[8,2,256]{2,1,0:T(2,128)} %all_to_all.69), calls=%async_computation.3 | async-start | bytes 32768 | tf_op jit(solution)/shard_map/all_to_all | solution.py:99
  101.5 9.9 %all-to-all-start.4 = ((f32[8,2,256]{2,1,0:T(2,128)}), f32[8,2,256]{2,1,0:T(2,128)S(1)}, u32[]{:S(2)}, u32[]{:S(2)}) async-start(f32[8,2,256]{2,1,0:T(2,128)} %copy.29), calls=%async_computation.4 | async-start | bytes 32768 | tf_op jit(solution)/shard_map/all_to_all | solution.py:117
  128.9 34.1 %all-to-all-start.5 = ((f32[8,2,256]{2,1,0:T(2,128)}), f32[8,2,256]{2,1,0:T(2,128)S(1)}, u32[]{:S(2)}, u32[]{:S(2)}) async-start(f32[8,2,256]{2,1,0:T(2,128)} %all_to_all.74), calls=%async_computation.5 | async-start | bytes 32768 | tf_op jit(solution)/shard_map/all_to_all | solution.py:99
  164.6 9.9 %all-to-all-start.6 = ((f32[8,2,256]{2,1,0:T(2,128)}), f32[8,2,256]{2,1,0:T(2,128)S(1)}, u32[]{:S(2)}, u32[]{:S(2)}) async-start(f32[8,2,256]{2,1,0:T(2,128)} %copy.30), calls=%async_computation.6 | async-start | bytes 32768 | tf_op jit(solution)/shard_map/all_to_all | solution.py:117
  192.0 34.2 %all-to-all-start.7 = ((f32[8,2,256]{2,1,0:T(2,128)}), f32[8,2,256]{2,1,0:T(2,128)S(1)}, u32[]{:S(2)}, u32[]{:S(2)}) async-start(f32[8,2,256]{2,1,0:T(2,128)} %all_to_all.79), calls=%async_computation.7 | async-start | bytes 32768 | tf_op jit(solution)/shard_map/all_to_all | solution.py:99
  227.3 35.0 %all-to-all-start.8 = ((f32[8,2,256]{2,1,0:T(2,128)}), f32[8,2,256]{2,1,0:T(2,128)S(1)}, u32[]{:S(2)}, u32[]{:S(2)}) async-start(f32[8,2,256]{2,1,0:T(2,128)} %copy.31), calls=%async_computation.8 | async-start | bytes 32768 | tf_op jit(solution)/shard_map/all_to_all | solution.py:117
